TPU v7x, 32 devices: a whole 2x2x4 slice. The times are simulated.
32 devices in a mesh: tp: 4 (over x, core), grp: 8 (over z, y).
Axes of the slice: x: 2, y: 2, z: 4, core: 2. Of those that a mesh axis runs over, the one named last changes fastest.
Arguments:
- flat_shards: bfloat16 [2, 2, 8256, 24576], P(None, None, ('grp', 'tp')), may hold values from -0.0625 to 0.0625
- offsets: int32 [2, 2], replicated, may hold values from 0 to 2
- probes: bfloat16 [512, 8192], P(None, 'grp'), may hold values from -6 to 6
Outputs:
- serving_tiles: bfloat16 [2, 2, 8192, 24576], P(None, None, 'grp', 'tp')
- hidden_check: bfloat16 [2, 512, 24576], P(None, 'grp', 'tp')
All inputs are finite; a program needn't handle non-finite values.
Results may differ from a plain program's by a relative error of at most 0.001.
Values may be sent and summed in bfloat16 or wider, within the bound.
A program may use at most 320 MiB of HBM per device.

v0:
```python
import jax
import jax.numpy as jnp
from jax import lax
from jax.sharding import PartitionSpec as P

PAD = 2


def per_device(flat_shards, offsets, probes):
    tp_count = lax.axis_size("tp")
    layer_count = flat_shards.shape[0]
    shard_rows = flat_shards.shape[2] - PAD
    columns = flat_shards.shape[3] // tp_count
    tile_layers = []
    check_layers = []
    for which_layer in range(layer_count):
        tiles = []
        sums = []
        for which_tensor in range(2):
            start = offsets[which_layer, which_tensor]
            picked = lax.dynamic_slice_in_dim(
                flat_shards[which_layer, which_tensor], start, shard_rows, 0
            )
            picked = picked.reshape(shard_rows, tp_count, columns).transpose(1, 0, 2)
            moved = lax.all_to_all(picked, "tp", split_axis=0, concat_axis=0, tiled=True)
            tile = moved.reshape(tp_count * shard_rows, columns)
            partial = jnp.dot(probes, tile, preferred_element_type=jnp.float32)
            sums.append(lax.psum_scatter(partial, "grp", scatter_dimension=0, tiled=True))
            tiles.append(tile)
        tile_layers.append(jnp.stack(tiles))
        check_layers.append((jax.nn.silu(sums[0]) * sums[1]).astype(jnp.bfloat16))
    return (jnp.stack(tile_layers), jnp.stack(check_layers))


def solution(mesh):
    placed = (P(None, None, ("grp", "tp"), None), P(), P(None, "grp"))
    return jax.shard_map(
        per_device,
        mesh=mesh,
        in_specs=placed,
        out_specs=(P(None, None, "grp", "tp"), P(None, "grp", "tp")),
        check_vma=False,
    )
```

profile of v0, /device:TPU:0, one launch (start us, length us, event | category | flops | bytes accessed | tf_op | source)
XLA Modules:
  0.0 1469.4 jit_solution(10663330344858529196)
XLA Ops:
  11.1 92.3 %fusion.2 = (bf16[1,1,258,24576]{3,1,2,0:T(2,128)(2,1)}, bf16[1,1,258,24576]{3,1,2,0:T(2,128)(2,1)}, bf16[1,1,258,24576]{3,1,2,0:T(2,128)(2,1)}, bf16[1,1,258,24576]{3,1,2,0:T(2,128)(2,1)}) fusion(bf16[2,2,258,24576]{3,1,2,0:T(2,128)(2,1)} %param.3), kind=kLoop, calls=%fused_computation.16 | loop fusion | bytes 101449728 | tf_op jit(solution)/shard_map/slice | solution.py:22
  104.6 84.4 %constant_dynamic-slice_fusion.2 = (bf16[1,1,256,24576]{3,1,2,0:T(2,128)(2,1)}, bf16[1,1,256,24576]{3,1,2,0:T(2,128)(2,1)}) fusion(bf16[1,1,258,24576]{3,1,2,0:T(2,128)(2,1)} %get-tuple-element.12, s32[]{:T(128)S(6)} %select_n.13, bf16[1,1,258,24576]{3,1,2,0:T(2,128)(2,1)} %get-tuple-element.10, s32[]{:T(128)S(6)} %select_n.12), kind=kLoop, calls=%fused_computation.14 | loop fusion | bytes 50331656 | tf_op jit(solution)/shard_map/dynamic_slice | solution.py:21
  189.0 49.2 %copy.48 = bf16[1,1,256,24576]{2,3,1,0:T(8,128)(2,1)} copy(bf16[1,1,256,24576]{3,1,2,0:T(2,128)(2,1)} %get-tuple-element.20) | data formatting | bytes 25165824
  238.3 148.1 %all_to_all.20 = bf16[4,256,6144]{1,2,0:T(8,128)(2,1)} all-to-all(bf16[4,256,6144]{1,2,0:T(8,128)(2,1)} %bitcast.60), channel_id=1, replica_groups=mesh['tp'=4,'grp'=8] {'tp'}, dimensions={0} | all-to-all | bytes 25165824 | tf_op jit(solution)/shard_map/all_to_all | solution.py:25
  386.3 16.6 %copy.27 = bf16[4,256,6144]{2,1,0:T(8,128)(2,1)} copy(bf16[4,256,6144]{1,2,0:T(8,128)(2,1)} %all_to_all.20) | data formatting | bytes 25165824 | tf_op jit(solution)/shard_map/all_to_all | solution.py:25
  403.0 14.4 convolution_bitcast_fusion.2
  417.4 12.7 copy.39
  430.2 49.4 %copy.46 = bf16[1,1,256,24576]{2,3,1,0:T(8,128)(2,1)} copy(bf16[1,1,256,24576]{3,1,2,0:T(2,128)(2,1)} %get-tuple-element.21) | data formatting | bytes 25165824
  479.6 147.5 %all_to_all.21 = bf16[4,256,6144]{1,2,0:T(8,128)(2,1)} all-to-all(bf16[4,256,6144]{1,2,0:T(8,128)(2,1)} %bitcast.61), channel_id=1, replica_groups=mesh['tp'=4,'grp'=8] {'tp'}, dimensions={0} | all-to-all | bytes 25165824 | tf_op jit(solution)/shard_map/all_to_all | solution.py:25
  627.1 16.6 %copy.25 = bf16[4,256,6144]{2,1,0:T(8,128)(2,1)} copy(bf16[4,256,6144]{1,2,0:T(8,128)(2,1)} %all_to_all.21) | data formatting | bytes 25165824 | tf_op jit(solution)/shard_map/all_to_all | solution.py:25
  643.7 14.4 convolution_bitcast_fusion.3
  674.7 84.4 %constant_dynamic-slice_fusion = (bf16[1,1,256,24576]{3,1,2,0:T(2,128)(2,1)}, bf16[1,1,256,24576]{3,1,2,0:T(2,128)(2,1)}) fusion(bf16[1,1,258,24576]{3,1,2,0:T(2,128)(2,1)} %get-tuple-element.13, s32[]{:T(128)S(6)} %select_n.15, bf16[1,1,258,24576]{3,1,2,0:T(2,128)(2,1)} %get-tuple-element.11, s32[]{:T(128)S(6)} %select_n.14), kind=kLoop, calls=%fused_computation.12 | loop fusion | bytes 50331656 | tf_op jit(solution)/shard_map/dynamic_slice | solution.py:21
  759.0 49.5 %copy.52 = bf16[1,1,256,24576]{2,3,1,0:T(8,128)(2,1)} copy(bf16[1,1,256,24576]{3,1,2,0:T(2,128)(2,1)} %get-tuple-element.18) | data formatting | bytes 25165824
  808.6 147.4 %all_to_all.22 = bf16[4,256,6144]{1,2,0:T(8,128)(2,1)} all-to-all(bf16[4,256,6144]{1,2,0:T(8,128)(2,1)} %bitcast.62), channel_id=1, replica_groups=mesh['tp'=4,'grp'=8] {'tp'}, dimensions={0} | all-to-all | bytes 25165824 | tf_op jit(solution)/shard_map/all_to_all | solution.py:25
  955.9 16.6 %copy.31 = bf16[4,256,6144]{2,1,0:T(8,128)(2,1)} copy(bf16[4,256,6144]{1,2,0:T(8,128)(2,1)} %all_to_all.22) | data formatting | bytes 25165824 | tf_op jit(solution)/shard_map/all_to_all | solution.py:25
  972.5 14.6 convolution_bitcast_fusion
  999.8 49.5 %copy.50 = bf16[1,1,256,24576]{2,3,1,0:T(8,128)(2,1)} copy(bf16[1,1,256,24576]{3,1,2,0:T(2,128)(2,1)} %get-tuple-element.19) | data formatting | bytes 25165824
  1049.3 147.4 %all_to_all.23 = bf16[4,256,6144]{1,2,0:T(8,128)(2,1)} all-to-all(bf16[4,256,6144]{1,2,0:T(8,128)(2,1)} %bitcast.63), channel_id=1, replica_groups=mesh['tp'=4,'grp'=8] {'tp'}, dimensions={0} | all-to-all | bytes 25165824 | tf_op jit(solution)/shard_map/all_to_all | solution.py:25
  1196.7 16.7 %copy.29 = bf16[4,256,6144]{2,1,0:T(8,128)(2,1)} copy(bf16[4,256,6144]{1,2,0:T(8,128)(2,1)} %all_to_all.23) | data formatting | bytes 25165824 | tf_op jit(solution)/shard_map/all_to_all | solution.py:25
  1213.4 14.5 convolution_bitcast_fusion.1
  1240.5 20.6 %maximum_bitcast_fusion = bf16[1,2,1024,6144]{3,2,1,0:T(8,128)(2,1)} fusion(bf16[1,1024,6144]{2,1,0:T(8,128)(2,1)} %bitcast.53, bf16[1,1024,6144]{2,1,0:T(8,128)(2,1)} %bitcast.55), kind=kLoop, calls=%fused_computation.1 | loop fusion | flops 12582912 | bytes 50331648 | tf_op jit(solution)/shard_map/stack | solution.py:32
  1261.1 20.6 %maximum_bitcast_fusion.1 = bf16[1,2,1024,6144]{3,2,1,0:T(8,128)(2,1)} fusion(bf16[1,1024,6144]{2,1,0:T(8,128)(2,1)} %bitcast.57, bf16[1,1024,6144]{2,1,0:T(8,128)(2,1)} %bitcast.59), kind=kLoop, calls=%fused_computation.2 | loop fusion | flops 12582912 | bytes 50331648 | tf_op jit(solution)/shard_map/stack | solution.py:32
  1281.7 33.4 %pad_maximum_fusion = bf16[2,2,1024,6144]{3,2,1,0:T(8,128)(2,1)} fusion(bf16[1,2,1024,6144]{3,2,1,0:T(8,128)(2,1)} %maximum_bitcast_fusion.1, bf16[1,2,1024,6144]{3,2,1,0:T(8,128)(2,1)} %maximum_bitcast_fusion), kind=kLoop, calls=%fused_computation | loop fusion | flops 25165824 | bytes 100663296 | tf_op jit(solution)/shard_map/stack | solution.py:32
  1328.9 120.4 %reduce-scatter.17.cloned.1.call-done = f32[64,6144]{1,0:T(8,128)} async-done(((f32[512,6144]{1,0:T(8,128)}), f32[64,6144]{1,0:T(8,128)}) %reduce-scatter.17.cloned.1.call-update) | async-done | bytes 1572880
  (25 shorter events, 66.9 us)
Async XLA Ops:
  7.2 395.8 %copy-start = (bf16[512,1024]{1,0:T(8,128)(2,1)S(1)}, bf16[512,1024]{1,0:T(8,128)(2,1)}, u32[]{:S(2)}) copy-start(bf16[512,1024]{1,0:T(8,128)(2,1)} %param.5) | copy-start | bytes 3145732
  7.2 1308.0 %reduce-scatter.15.cloned.1.call-start = ((), (), s32[]{:S(2)}) async-start(), calls=%async_computation.9 | async-start | bytes 14155776
  430.1 888.3 %reduce-scatter.13.cloned.1.call-start = ((), (), s32[]{:S(2)}) async-start(), calls=%async_computation.8 | async-start | bytes 14155776
  670.8 651.0 %reduce-scatter.19.cloned.1.call-start = ((), (), s32[]{:S(2)}) async-start(), calls=%async_computation.11 | async-start | bytes 14155776
  999.7 449.6 %reduce-scatter.17.cloned.1.call-start = ((), (), s32[]{:S(2)}) async-start(), calls=%async_computation.10 | async-start | bytes 14155776
Sparse Core Ops, SparseCore 0:
  430.2 208.4 reduce-scatter.14
  671.0 208.5 reduce-scatter.12
  999.8 208.4 reduce-scatter.18
  1240.7 208.5 reduce-scatter.16
where the time goes:
time: 1480 us; the launch traced here: 1470 us
  local copies, waits for them, and re-layouts  595 us (40%)
  blocking collectives  590 us (40%)
  waiting for transfers between devices  120 us (8%)
  other arithmetic  84.4 us (6%)
  matrix products  57.9 us (4%)
  between operations  21.2 us (1%)
    all_to_all x4, blocking collectives, per_device(): lax.all_to_all(picked, 'tp', split_axis=0, concat_axis=0, tiled=True)  590 us
    unnamed x15, local copies, waits for them, and re-layouts  266 us
    dynamic_slice x2, local copies, waits for them, and re-layouts, per_device(): lax.dynamic_slice_in_dim(flat_shards[which_layer, which_tensor], start, s...  169 us
    unnamed x8, waiting for transfers between devices  120 us
    slice x1, local copies, waits for them, and re-layouts, per_device(): flat_shards[which_layer, which_tensor]  92.3 us
    another operation x6, other arithmetic, per_device(): return (jnp.stack(tile_layers), jnp.stack(check_layers))  84.4 us
    all_to_all x4, local copies, waits for them, and re-layouts, per_device(): lax.all_to_all(picked, 'tp', split_axis=0, concat_axis=0, tiled=True)  66.5 us
    dot_general x4, matrix products, per_device(): partial = jnp.dot(probes, tile, preferred_element_type=jnp.float32)  57.9 us
  transfers between devices with their start and end apart: 4, of which 1 were waited for; matrix products, arithmetic and copies ran while one was open for 31% of the time, Pallas kernels for 0%

commit v1 on v0

v1 whole, which is shorter than its diff:
```python
import functools

import jax
import jax.numpy as jnp
from jax import lax
from jax.experimental import pallas as pl
from jax.experimental.pallas import tpu as pltpu
from jax.sharding import PartitionSpec as P

PAD = 2
CHUNK = 512
SLOTS = 6
MESH = pl.DeviceIdType.MESH


def ring_device(place, count):
    half = count // 2
    back = lax.div(place, half)
    return (1 - back) * 2 * place + back * (2 * (count - 1 - place) + 1)


def exchange(
    tp_count,
    grp_count,
    flat_ref,
    tails_ref,
    main_ref,
    rest_ref,
    raw_ref,
    ends_ref,
    check_ref,
    xbuf,
    tailbuf,
    partial,
    outgoing,
    incoming,
    gate_sums,
    x_send,
    x_recv,
    x_free,
    own_sem,
    raw_sem,
    tail_send,
    tail_recv,
    tail_own,
    ends_sem,
    ring_send,
    ring_recv,
    ring_free,
):
    t = lax.axis_index("tp")
    g = lax.axis_index("grp")
    odd = lax.rem(g, 2)
    place = (1 - odd) * lax.div(g, 2) + odd * (grp_count - 1 - lax.div(g, 2))
    after = ring_device(lax.rem(place + 1, grp_count), grp_count)
    before = ring_device(lax.rem(place + grp_count - 1, grp_count), grp_count)
    toward = (after, before)
    origin = (before, after)

    pair_count = flat_ref.shape[0]
    rows = xbuf.shape[1] // tp_count
    columns = raw_ref.shape[2]
    chunk = xbuf.shape[2]
    per_layer = columns // chunk * 2
    total = columns // chunk * pair_count
    share = main_ref.shape[1] // grp_count
    half = share // 2
    hops = grp_count - 1

    def spot(index):
        layer = lax.div(index, per_layer)
        inside = lax.rem(index, per_layer)
        return layer * 2 + lax.rem(inside, 2), lax.div(inside, 2)

    def x_copy(index, step):
        pair, block = spot(index)
        slot = lax.rem(index, SLOTS)
        partner = lax.rem(t + step, tp_count)
        start = pl.multiple_of(partner * columns + block * chunk, chunk)
        return pltpu.make_async_remote_copy(
            src_ref=flat_ref.at[pair, pl.ds(0, rows), pl.ds(start, chunk)],
            dst_ref=xbuf.at[slot, pl.ds(pl.multiple_of(t * rows, rows), rows), :],
            send_sem=x_send.at[step - 1, slot],
            recv_sem=x_recv.at[step - 1, slot],
            device_id=(partner, g),
            device_id_type=MESH,
        )

    def x_arrival(index, step):
        slot = lax.rem(index, SLOTS)
        source = lax.rem(t + tp_count - step, tp_count)
        landing = xbuf.at[slot, pl.ds(pl.multiple_of(source * rows, rows), rows), :]
        return pltpu.make_async_remote_copy(
            src_ref=landing,
            dst_ref=landing,
            send_sem=x_send.at[step - 1, slot],
            recv_sem=x_recv.at[step - 1, slot],
            device_id=(source, g),
            device_id_type=MESH,
        )

    def own_copy(index):
        pair, block = spot(index)
        slot = lax.rem(index, SLOTS)
        start = pl.multiple_of(t * columns + block * chunk, chunk)
        return pltpu.make_async_copy(
            flat_ref.at[pair, pl.ds(0, rows), pl.ds(start, chunk)],
            xbuf.at[slot, pl.ds(pl.multiple_of(t * rows, rows), rows), :],
            own_sem.at[slot],
        )

    def raw_copy(index):
        pair, block = spot(index)
        slot = lax.rem(index, SLOTS)
        return pltpu.make_async_copy(
            xbuf.at[slot],
            raw_ref.at[pair, :, pl.ds(pl.multiple_of(block * chunk, chunk), chunk)],
            raw_sem.at[slot],
        )

    def tail_copy(step):
        partner = lax.rem(t + step, tp_count)
        return pltpu.make_async_remote_copy(
            src_ref=tails_ref.at[:, pl.ds(pl.multiple_of(partner * columns, chunk), columns)],
            dst_ref=tailbuf.at[t],
            send_sem=tail_send.at[step - 1],
            recv_sem=tail_recv.at[step - 1],
            device_id=(partner, g),
            device_id_type=MESH,
        )

    def tail_arrival(step):
        source = lax.rem(t + tp_count - step, tp_count)
        return pltpu.make_async_remote_copy(
            src_ref=tailbuf.at[source],
            dst_ref=tailbuf.at[source],
            send_sem=tail_send.at[step - 1],
            recv_sem=tail_recv.at[step - 1],
            device_id=(source, g),
            device_id_type=MESH,
        )

    def ring_copy(way, stage, turn):
        return pltpu.make_async_remote_copy(
            src_ref=outgoing.at[way, stage, turn],
            dst_ref=incoming.at[way, stage, turn],
            send_sem=ring_send.at[way, stage, turn],
            recv_sem=ring_recv.at[way, stage, turn],
            device_id=(t, toward[way]),
            device_id_type=MESH,
        )

    def own_rows(way, stage):
        if way == 0:
            owner = lax.rem(place + 2 * grp_count - 1 - stage, grp_count)
        else:
            owner = lax.rem(place + 1 + stage, grp_count)
        first = ring_device(owner, grp_count) * share + way * half
        return pl.ds(pl.multiple_of(first, half), half)

    barrier = pltpu.get_barrier_semaphore()
    for step in range(1, tp_count):
        pl.semaphore_signal(
            barrier, inc=1, device_id=(lax.rem(t + step, tp_count), g), device_id_type=MESH
        )
    for way in range(2):
        pl.semaphore_signal(barrier, inc=1, device_id=(t, toward[way]), device_id_type=MESH)
    pl.semaphore_wait(barrier, tp_count - 1 + 2)

    for step in range(1, tp_count):
        tail_copy(step).start()
    own_tail = pltpu.make_async_copy(
        tails_ref.at[:, pl.ds(pl.multiple_of(t * columns, chunk), columns)],
        tailbuf.at[t],
        tail_own,
    )
    own_tail.start()

    @pl.loop(0, SLOTS - 1)
    def _(index):
        for step in range(1, tp_count):
            x_copy(index, step).start()
        own_copy(index).start()

    own_tail.wait()
    for step in range(1, tp_count):
        tail_arrival(step).wait_recv()
    ends = pltpu.make_async_copy(tailbuf, ends_ref, ends_sem)
    ends.start()

    @pl.loop(0, total + hops)
    def _(tick):
        turn = lax.rem(tick, 2)
        last_turn = 1 - turn

        @pl.when(jnp.logical_and(tick >= 2, tick < total + hops - 1))
        def _():
            for way in range(2):
                pl.semaphore_wait(ring_free.at[way], 1)

        for stage in range(hops, 0, -1):
            index = tick - stage

            @pl.when(jnp.logical_and(index >= 0, index < total))
            def _():
                place_of = lax.rem(index, grp_count)
                if stage < hops:

                    @pl.when(index >= 2)
                    def _():
                        for way in range(2):
                            ring_copy(way, stage, turn).wait_send()

                    for way in range(2):
                        ring_copy(way, stage - 1, last_turn).wait_recv()
                        outgoing[way, stage, turn] = (
                            incoming[way, stage - 1, last_turn]
                            + partial[place_of, own_rows(way, stage), :]
                        )
                        ring_copy(way, stage, turn).start()
                else:
                    pair, block = spot(index)
                    parts = []
                    for way in range(2):
                        ring_copy(way, stage - 1, last_turn).wait_recv()
                        parts.append(
                            incoming[way, stage - 1, last_turn]
                            + partial[place_of, own_rows(way, stage), :]
                        )
                    sums = jnp.concatenate(parts, axis=0)

                    @pl.when(lax.rem(pair, 2) == 0)
                    def _():
                        gate_sums[...] = sums

                    @pl.when(lax.rem(pair, 2) == 1)
                    def _():
                        gate = gate_sums[...]
                        hidden = gate / (1.0 + jnp.exp(-gate)) * sums
                        where = pl.ds(pl.multiple_of(block * chunk, chunk), chunk)
                        check_ref[lax.div(pair, 2), :, where] = hidden.astype(check_ref.dtype)

        @pl.when(tick < total)
        def _():
            slot = lax.rem(tick, SLOTS)
            kept = lax.rem(tick, grp_count)
            pair, block = spot(tick)
            own_copy(tick).wait()
            for step in range(1, tp_count):
                x_arrival(tick, step).wait_recv()
            raw_copy(tick).start()
            where = pl.ds(pl.multiple_of(block * chunk, chunk), chunk)
            tail = tailbuf[:, :, where].reshape(tp_count * tailbuf.shape[1], chunk)
            partial[kept] = jnp.dot(
                main_ref[pair], xbuf[slot], preferred_element_type=jnp.float32
            ) + jnp.dot(rest_ref[pair], tail, preferred_element_type=jnp.float32)

            @pl.when(tick >= 2)
            def _():
                for way in range(2):
                    ring_copy(way, 0, turn).wait_send()

            for way in range(2):
                outgoing[way, 0, turn] = partial[kept, own_rows(way, 0), :]
                ring_copy(way, 0, turn).start()

        @pl.when(jnp.logical_and(tick >= 1, tick < total + hops - 2))
        def _():
            for way in range(2):
                pl.semaphore_signal(
                    ring_free.at[way], inc=1, device_id=(t, origin[way]), device_id_type=MESH
                )

        @pl.when(jnp.logical_and(tick >= 1, tick < total + 1))
        def _():
            raw_copy(tick - 1).wait()

        ahead = tick + SLOTS - 1

        @pl.when(jnp.logical_and(tick >= 1, ahead < total))
        def _():
            for step in range(1, tp_count):
                pl.semaphore_signal(
                    x_free.at[step - 1],
                    inc=1,
                    device_id=(lax.rem(t + tp_count - step, tp_count), g),
                    device_id_type=MESH,
                )

        @pl.when(ahead < total)
        def _():
            @pl.when(tick >= 1)
            def _():
                for step in range(1, tp_count):
                    x_copy(ahead - SLOTS, step).wait_send()
                    pl.semaphore_wait(x_free.at[step - 1], 1)

            for step in range(1, tp_count):
                x_copy(ahead, step).start()
            own_copy(ahead).start()

    @pl.loop(total - SLOTS, total)
    def _(index):
        for step in range(1, tp_count):
            x_copy(index, step).wait_send()

    for stage in range(hops):
        for way in range(2):
            for turn in range(2):
                ring_copy(way, stage, turn).wait_send()
    for step in range(1, tp_count):
        tail_copy(step).wait_send()
    ends.wait()


def align(pair_tails, offsets_ref, raw_ref, ends_ref, tile_ref):
    pair = pl.program_id(0)
    start = offsets_ref[pair]
    rows, width = tile_ref.shape[1:]
    step = 256
    count = ends_ref.shape[1]

    @pl.when(start == 0)
    def _():
        tile_ref[...] = raw_ref[...]

    for shift in range(1, pair_tails + 1):

        @pl.when(start == shift)
        def _():
            @pl.loop(0, width // step)
            def _(at):
                where = pl.ds(pl.multiple_of(at * step, step), step)
                raw = raw_ref[0, :, where].astype(jnp.float32)
                ends = ends_ref[0, :, where].astype(jnp.float32)
                ends = pltpu.roll(ends, lax.rem(count - pair_tails * pair, count), 0)
                joined = jnp.concatenate([raw, ends], axis=0)
                tile_ref[0, :, where] = joined[shift : shift + rows].astype(tile_ref.dtype)


def per_device(flat_shards, offsets, probes):
    tp_count = lax.axis_size("tp")
    grp_count = lax.axis_size("grp")
    layers, tensors, shard, width = flat_shards.shape
    pairs = layers * tensors
    rows = shard - PAD
    columns = width // tp_count
    probe_count = probes.shape[0]
    chunk = CHUNK
    share = probe_count // grp_count
    half = share // 2
    hops = grp_count - 1

    starts = offsets.reshape(pairs)
    spread = jnp.pad(probes.reshape(probe_count, tp_count, rows), ((0, 0), (0, 0), (PAD, PAD)))
    shifts = [spread[:, :, PAD - shift : PAD - shift + shard] for shift in range(PAD + 1)]
    mains, rests = [], []
    for pair in range(pairs):
        moved = shifts[0]
        for shift in range(1, PAD + 1):
            moved = jnp.where(starts[pair] == shift, shifts[shift], moved)
        mains.append(moved[:, :, :rows].reshape(probe_count, tp_count * rows))
        sides = ((0, 0), (0, 0), (pair * PAD, (pairs - 1 - pair) * PAD))
        rests.append(jnp.pad(moved[:, :, rows:], sides).reshape(probe_count, tp_count * pairs * PAD))
    main, rest = jnp.stack(mains), jnp.stack(rests)
    flat = flat_shards.reshape(pairs, shard, width)
    tails = flat[:, rows:, :].reshape(pairs * PAD, width)

    anywhere = pl.BlockSpec(memory_space=pl.ANY)
    inside = pl.BlockSpec(memory_space=pltpu.VMEM)
    dma = pltpu.SemaphoreType.DMA
    regular = pltpu.SemaphoreType.REGULAR
    raw, ends, check = pl.pallas_call(
        functools.partial(exchange, tp_count, grp_count),
        out_shape=(
            jax.ShapeDtypeStruct((pairs, tp_count * rows, columns), flat.dtype),
            jax.ShapeDtypeStruct((tp_count, pairs * PAD, columns), flat.dtype),
            jax.ShapeDtypeStruct((layers, share, columns), jnp.bfloat16),
        ),
        in_specs=[anywhere, anywhere, inside, inside],
        out_specs=(anywhere, anywhere, inside),
        scratch_shapes=[
            pltpu.VMEM((SLOTS, tp_count * rows, chunk), flat.dtype),
            pltpu.VMEM((tp_count, pairs * PAD, columns), flat.dtype),
            pltpu.VMEM((grp_count, probe_count, chunk), jnp.float32),
            pltpu.VMEM((2, hops, 2, half, chunk), jnp.float32),
            pltpu.VMEM((2, hops, 2, half, chunk), jnp.float32),
            pltpu.VMEM((share, chunk), jnp.float32),
            dma((tp_count - 1, SLOTS)),
            dma((tp_count - 1, SLOTS)),
            regular((tp_count - 1,)),
            dma((SLOTS,)),
            dma((SLOTS,)),
            dma((tp_count - 1,)),
            dma((tp_count - 1,)),
            dma,
            dma,
            dma((2, hops, 2)),
            dma((2, hops, 2)),
            regular((2,)),
        ],
        compiler_params=pltpu.CompilerParams(
            collective_id=0, has_side_effects=True, vmem_limit_bytes=60 * 1024 * 1024
        ),
    )(flat, tails, main, rest)

    block = columns // 2
    tiles = pl.pallas_call(
        functools.partial(align, PAD),
        out_shape=jax.ShapeDtypeStruct((pairs, tp_count * rows, columns), flat.dtype),
        grid_spec=pltpu.PrefetchScalarGridSpec(
            num_scalar_prefetch=1,
            grid=(pairs, tp_count, columns // block),
            in_specs=[
                pl.BlockSpec((1, rows, block), lambda p, s, b, starts: (p, s, b)),
                pl.BlockSpec((1, pairs * PAD, block), lambda p, s, b, starts: (s, 0, b)),
            ],
            out_specs=pl.BlockSpec((1, rows, block), lambda p, s, b, starts: (p, s, b)),
        ),
    )(starts, raw, ends)
    return tiles.reshape(layers, tensors, tp_count * rows, columns), check


def solution(mesh):
    placed = (P(None, None, ("grp", "tp"), None), P(), P(None, "grp"))
    return jax.shard_map(
        per_device,
        mesh=mesh,
        in_specs=placed,
        out_specs=(P(None, None, "grp", "tp"), P(None, "grp", "tp")),
        check_vma=False,
    )
```

time: 1480 us -> 708 us (0.48)
  Pallas kernels: 0 us -> 634 us
  blocking collectives: 590 us -> 0 us
  local copies, waits for them, and re-layouts: 595 us -> 53.4 us
  waiting for transfers between devices: 120 us -> 0 us
  other arithmetic: 84.4 us -> 13.2 us
  matrix products: 57.9 us -> 0 us
  between operations: 21.2 us -> 5.88 us
    pallas_call x0 -> x2, Pallas kernels: none -> 634 us  [the longest x1 586 us: per_device(): pl.pallas_call(functools.partial(exchange, tp_count, grp_count), out_shap...]
    all_to_all x4 -> x0, blocking collectives: 590 us -> none  [per_device(): lax.all_to_all(picked, 'tp', split_axis=0, concat_axis=0, tiled=True)]
    unnamed x15 -> x11, local copies, waits for them, and re-layouts: 266 us -> 38.9 us
    dynamic_slice x2 -> x0, local copies, waits for them, and re-layouts: 169 us -> none  [per_device(): lax.dynamic_slice_in_dim(flat_shards[which_layer, which_tensor], start, s...]
    unnamed x8 -> x0, waiting for transfers between devices: 120 us -> none
    slice x2 -> x10, local copies, waits for them, and re-layouts: 93.8 us -> 4.57 us  [the longest x4 2.32 us: per_device(): mains.append(moved[:, :, :rows].reshape(probe_count, tp_count * rows))]
    another operation x6 -> x2, other arithmetic: 84.4 us -> 3.49 us  [per_device(): main, rest = (jnp.stack(mains), jnp.stack(rests))]
    all_to_all x4 -> x0, local copies, waits for them, and re-layouts: 66.5 us -> none  [per_device(): lax.all_to_all(picked, 'tp', split_axis=0, concat_axis=0, tiled=True)]
  transfers between devices with their start and end apart: 4 -> 0, of which waited for: 1 -> 0; matrix products, arithmetic and copies ran while one was open for 31% -> 0% of each run, Pallas kernels for 0% -> 0%
where the time goes in v1:
time: 708 us; the launch traced here: 706 us
  Pallas kernels  634 us (90%)
  local copies, waits for them, and re-layouts  53.4 us (8%)
  other arithmetic  13.2 us (2%)
    pallas_call x1, Pallas kernels, per_device(): pl.pallas_call(functools.partial(exchange, tp_count, grp_count), out_shap...  586 us
    pallas_call x1, Pallas kernels, per_device(): pl.pallas_call(functools.partial(align, PAD), out_shape=jax.ShapeDtypeStr...  47.8 us
    unnamed x11, local copies, waits for them, and re-layouts  38.9 us

profile of v1, /device:TPU:0, one launch (start us, length us, event | category | flops | bytes accessed | tf_op | source)
XLA Modules:
  0.0 706.2 jit_solution(4622691237698338725)
XLA Ops:
  0.6 0.8 reshape.35.offsets_ref
  1.4 0.6 fusion
  7.1 2.3 copy.17
  9.4 9.7 %select_select_fusion.3 = (bf16[512,4,258]{0,2,1:T(8,128)(2,1)S(1)}, bf16[512,4,258]{0,2,1:T(8,128)(2,1)S(1)}, bf16[512,4,258]{0,2,1:T(8,128)(2,1)S(1)}, bf16[512,4,258]{0,2,1:T(8,128)(2,1)S(1)}) fusion(pred[]{:T(512)} %bitcast.3, pred[]{:T(512)} %bitcast.1, bf16[512,4,256]{0,2,1:T(8,128)(2,1)} %bitcast.30, pred[]{:T(512)} %bitcast.12, pred[]{:T(512)} %bitcast.11, ...), kind=kLoop, calls=%fused_computation.4 | loop fusion | flops 4227072 | bytes 5275656 | tf_op jit(solution)/shard_map/jit(_where)/select_n | solution.py:361
  19.1 0.0 copy-done.3
  19.2 1.1 slice.69
  20.2 2.3 copy.23
  22.5 1.1 slice.72
  23.6 2.3 copy.26
  25.9 0.1 slice.70
  26.0 1.3 copy.24
  27.3 0.1 slice.71
  27.4 0.0 copy-start
  27.4 0.0 copy-start.1
  27.4 1.3 copy.25
  28.7 0.6 copy-done.1
  29.3 3.5 pad_maximum_fusion.main_ref
  32.9 1.0 copy.22.rest_ref
  33.9 34.9 %copy.16 = bf16[2,2,258,24576]{3,2,1,0:T(8,128)(2,1)} copy(bf16[2,2,258,24576]{3,1,2,0:T(2,128)(2,1)} %param.3) | data formatting | bytes 101449728 | tf_op args[0]
  68.8 1.6 slice.68
  70.4 0.9 reshape.37.tails_ref
  71.3 585.9 %shard_map.50 = (bf16[4,1024,6144]{2,1,0:T(8,128)(2,1)}, bf16[4,8,6144]{2,1,0:T(8,128)(2,1)}, bf16[2,64,6144]{2,1,0:T(8,128)(2,1)}) custom-call(bf16[4,258,24576]{2,1,0:T(8,128)(2,1)} %bitcast.24, bf16[8,24576]{1,0:T(8,128)(2,1)} %reshape.37.tails_ref, bf16[4,512,1024]{2,1,0:T(8,128)(2,1)} %pad_maximum_fusion.main_ref, bf16[4,512,32]{2,1,0:T(8,128)(2,1)} %copy.22.rest_ref), custom_call_target="tpu_custom_call" | custom-call | tf_op jit(solution)/shard_map/pallas_call | solution.py:373
  657.2 47.8 %shard_map.51 = bf16[4,1024,6144]{2,1,0:T(8,128)(2,1)} custom-call(s32[4]{0:T(128)} %copy-done.3, bf16[4,1024,6144]{2,1,0:T(8,128)(2,1)} %get-tuple-element.5.raw_ref, bf16[4,8,6144]{2,1,0:T(8,128)(2,1)} %get-tuple-element.6.ends_ref), custom_call_target="tpu_custom_call" | custom-call | tf_op jit(solution)/shard_map/pallas_call | solution.py:408
  705.0 1.1 copy.28
  (11 shorter events, 0.1 us)
Async XLA Ops:
  1.4 17.8 %copy-start.3 = (s32[4]{0:T(128)}, s32[4]{0:T(128)S(1)}, u32[]{:S(2)}) copy-start(s32[4]{0:T(128)S(1)} %reshape.35.offsets_ref) | copy-start | bytes 52
  27.4 1.3 copy-start
  27.4 1.9 copy-start.1
  657.2 47.9 %copy-start.2 = (bf16[2,64,6144]{2,1,0:T(8,128)(2,1)S(1)}, bf16[2,64,6144]{2,1,0:T(8,128)(2,1)}, u32[]{:S(2)}) copy-start(bf16[2,64,6144]{2,1,0:T(8,128)(2,1)} %get-tuple-element.23) | copy-start | bytes 4718596

commit v2 on v1

v2 whole, which is shorter than its diff:
```python
import functools

import jax
import jax.numpy as jnp
from jax import lax
from jax.experimental import pallas as pl
from jax.experimental.pallas import tpu as pltpu
from jax.sharding import PartitionSpec as P

PAD = 2
WIDTH = 256
LANES = 128
SLOTS = 4
MESH = pl.DeviceIdType.MESH


def ring_device(place, count):
    half = count // 2
    back = lax.div(place, half)
    return (1 - back) * 2 * place + back * (2 * (count - 1 - place) + 1)


def exchange(
    tp_count,
    grp_count,
    flat_ref,
    offsets_ref,
    probes_ref,
    raw_ref,
    check_ref,
    inbuf,
    chosen,
    sending,
    xbuf,
    partial,
    outgoing,
    incoming,
    in_sem,
    x_send,
    x_recv,
    x_free,
    raw_sem,
    ring_send,
    ring_recv,
    ring_free,
):
    t = lax.axis_index("tp")
    g = lax.axis_index("grp")
    odd = lax.rem(g, 2)
    place = (1 - odd) * lax.div(g, 2) + odd * (grp_count - 1 - lax.div(g, 2))
    after = ring_device(lax.rem(place + 1, grp_count), grp_count)
    before = ring_device(lax.rem(place + grp_count - 1, grp_count), grp_count)
    toward = (after, before)
    origin = (before, after)

    layers, shard, tensors, _ = flat_ref.shape
    rows = shard - PAD
    columns = raw_ref.shape[3]
    chunk = xbuf.shape[2]
    width = chunk // tensors
    per_layer = columns // width
    total = layers * per_layer
    share = probes_ref.shape[0] // grp_count
    half = share // 2
    hops = grp_count - 1

    def fetch(index, step, piece):
        layer, block = lax.div(index, per_layer), lax.rem(index, per_layer)
        turn = lax.rem(index, 2)
        partner = lax.rem(t + step, tp_count)
        start = pl.multiple_of(partner * columns + block * width + piece * LANES, LANES)
        return pltpu.make_async_copy(
            flat_ref.at[layer, :, :, pl.ds(start, LANES)],
            inbuf.at[turn, step, piece],
            in_sem.at[turn, step, piece],
        )

    def fetch_all(index):
        for step in range(tp_count):
            for piece in range(width // LANES):
                fetch(index, step, piece).start()

    def choose(index):
        layer = lax.div(index, per_layer)
        turn, slot = lax.rem(index, 2), lax.rem(index, SLOTS)
        for step in list(range(1, tp_count)) + [0]:
            pieces = []
            for piece in range(width // LANES):
                fetch(index, step, piece).wait()
                pieces.append(inbuf[turn, step, piece].reshape(shard * tensors, LANES))
            both = jnp.concatenate(pieces, axis=1)
            for tensor in range(tensors):
                picked = jnp.dot(
                    chosen[layer * tensors + tensor], both, preferred_element_type=jnp.float32
                ).astype(xbuf.dtype)
                where = slice(tensor * width, (tensor + 1) * width)
                if step == 0:
                    xbuf[slot, pl.ds(pl.multiple_of(t * rows, rows), rows), where] = picked
                else:
                    sending[slot, step - 1, :, where] = picked

    def x_copy(index, step):
        slot = lax.rem(index, SLOTS)
        return pltpu.make_async_remote_copy(
            src_ref=sending.at[slot, step - 1],
            dst_ref=xbuf.at[slot, pl.ds(pl.multiple_of(t * rows, rows), rows), :],
            send_sem=x_send.at[step - 1, slot],
            recv_sem=x_recv.at[step - 1, slot],
            device_id=(lax.rem(t + step, tp_count), g),
            device_id_type=MESH,
        )

    def x_arrival(index, step):
        slot = lax.rem(index, SLOTS)
        source = lax.rem(t + tp_count - step, tp_count)
        landing = xbuf.at[slot, pl.ds(pl.multiple_of(source * rows, rows), rows), :]
        return pltpu.make_async_remote_copy(
            src_ref=landing,
            dst_ref=landing,
            send_sem=x_send.at[step - 1, slot],
            recv_sem=x_recv.at[step - 1, slot],
            device_id=(source, g),
            device_id_type=MESH,
        )

    def raw_copy(index, tensor):
        layer, block = lax.div(index, per_layer), lax.rem(index, per_layer)
        slot = lax.rem(index, SLOTS)
        where = pl.ds(pl.multiple_of(block * width, width), width)
        return pltpu.make_async_copy(
            xbuf.at[slot, :, pl.ds(tensor * width, width)],
            raw_ref.at[layer, tensor, :, where],
            raw_sem.at[slot, tensor],
        )

    def ring_copy(way, stage, turn):
        return pltpu.make_async_remote_copy(
            src_ref=outgoing.at[way, stage, turn],
            dst_ref=incoming.at[way, stage, turn],
            send_sem=ring_send.at[way, stage, turn],
            recv_sem=ring_recv.at[way, stage, turn],
            device_id=(t, toward[way]),
            device_id_type=MESH,
        )

    def own_rows(way, stage):
        if way == 0:
            owner = lax.rem(place + 2 * grp_count - 1 - stage, grp_count)
        else:
            owner = lax.rem(place + 1 + stage, grp_count)
        first = ring_device(owner, grp_count) * share + way * half
        return pl.ds(pl.multiple_of(first, half), half)

    fetch_all(0)
    fetch_all(1)
    at_row = lax.broadcasted_iota(jnp.int32, (rows, shard * tensors), 0)
    at_column = lax.broadcasted_iota(jnp.int32, (rows, shard * tensors), 1)
    for layer in range(layers):
        for tensor in range(tensors):
            wanted = (at_row + offsets_ref[layer, tensor]) * tensors + tensor
            chosen[layer * tensors + tensor] = jnp.where(at_column == wanted, 1.0, 0.0).astype(
                chosen.dtype
            )

    barrier = pltpu.get_barrier_semaphore()
    for step in range(1, tp_count):
        pl.semaphore_signal(
            barrier, inc=1, device_id=(lax.rem(t + step, tp_count), g), device_id_type=MESH
        )
    for way in range(2):
        pl.semaphore_signal(barrier, inc=1, device_id=(t, toward[way]), device_id_type=MESH)
    pl.semaphore_wait(barrier, tp_count - 1 + 2)

    @pl.loop(0, SLOTS - 1)
    def _(index):
        choose(index)
        for step in range(1, tp_count):
            x_copy(index, step).start()
        fetch_all(index + 2)

    @pl.loop(0, total + hops)
    def _(tick):
        turn = lax.rem(tick, 2)
        last_turn = 1 - turn

        @pl.when(jnp.logical_and(tick >= 2, tick < total + hops - 1))
        def _():
            for way in range(2):
                pl.semaphore_wait(ring_free.at[way], 1)

        for stage in range(hops, 0, -1):
            index = tick - stage

            @pl.when(jnp.logical_and(index >= 0, index < total))
            def _():
                place_of = lax.rem(index, grp_count)
                if stage < hops:

                    @pl.when(index >= 2)
                    def _():
                        for way in range(2):
                            ring_copy(way, stage, turn).wait_send()

                    for way in range(2):
                        ring_copy(way, stage - 1, last_turn).wait_recv()
                        outgoing[way, stage, turn] = (
                            incoming[way, stage - 1, last_turn]
                            + partial[place_of, own_rows(way, stage), :]
                        )
                        ring_copy(way, stage, turn).start()
                else:
                    layer, block = lax.div(index, per_layer), lax.rem(index, per_layer)
                    parts = []
                    for way in range(2):
                        ring_copy(way, stage - 1, last_turn).wait_recv()
                        parts.append(
                            incoming[way, stage - 1, last_turn]
                            + partial[place_of, own_rows(way, stage), :]
                        )
                    sums = jnp.concatenate(parts, axis=0)
                    gate, up = sums[:, :width], sums[:, width:]
                    hidden = gate / (1.0 + jnp.exp(-gate)) * up
                    where = pl.ds(pl.multiple_of(block * width, width), width)
                    check_ref[layer, :, where] = hidden.astype(check_ref.dtype)

        @pl.when(tick < total)
        def _():
            slot = lax.rem(tick, SLOTS)
            kept = lax.rem(tick, grp_count)
            for step in range(1, tp_count):
                x_arrival(tick, step).wait_recv()
            for tensor in range(tensors):
                raw_copy(tick, tensor).start()
            partial[kept] = jnp.dot(
                probes_ref[...], xbuf[slot], preferred_element_type=jnp.float32
            )

            @pl.when(tick >= 2)
            def _():
                for way in range(2):
                    ring_copy(way, 0, turn).wait_send()

            for way in range(2):
                outgoing[way, 0, turn] = partial[kept, own_rows(way, 0), :]
                ring_copy(way, 0, turn).start()

        @pl.when(jnp.logical_and(tick >= 1, tick < total + hops - 2))
        def _():
            for way in range(2):
                pl.semaphore_signal(
                    ring_free.at[way], inc=1, device_id=(t, origin[way]), device_id_type=MESH
                )

        @pl.when(jnp.logical_and(tick >= 1, tick < total + 1))
        def _():
            for tensor in range(tensors):
                raw_copy(tick - 1, tensor).wait()

        ahead = tick + SLOTS - 1

        @pl.when(jnp.logical_and(tick >= 1, ahead < total))
        def _():
            for step in range(1, tp_count):
                pl.semaphore_signal(
                    x_free.at[step - 1],
                    inc=1,
                    device_id=(lax.rem(t + tp_count - step, tp_count), g),
                    device_id_type=MESH,
                )

        @pl.when(ahead < total)
        def _():
            @pl.when(tick >= 1)
            def _():
                for step in range(1, tp_count):
                    x_copy(ahead - SLOTS, step).wait_send()

            choose(ahead)

            @pl.when(tick >= 1)
            def _():
                for step in range(1, tp_count):
                    pl.semaphore_wait(x_free.at[step - 1], 1)

            for step in range(1, tp_count):
                x_copy(ahead, step).start()

            @pl.when(ahead + 2 < total)
            def _():
                fetch_all(ahead + 2)

    @pl.loop(total - SLOTS, total)
    def _(index):
        for step in range(1, tp_count):
            x_copy(index, step).wait_send()

    for stage in range(hops):
        for way in range(2):
            for turn in range(2):
                ring_copy(way, stage, turn).wait_send()


def per_device(flat_shards, offsets, probes):
    tp_count = lax.axis_size("tp")
    grp_count = lax.axis_size("grp")
    layers, tensors, shard, total_width = flat_shards.shape
    pairs = layers * tensors
    rows = shard - PAD
    columns = total_width // tp_count
    probe_count = probes.shape[0]
    chunk = tensors * WIDTH
    share = probe_count // grp_count
    half = share // 2
    hops = grp_count - 1

    anywhere = pl.BlockSpec(memory_space=pl.ANY)
    inside = pl.BlockSpec(memory_space=pltpu.VMEM)
    dma = pltpu.SemaphoreType.DMA
    regular = pltpu.SemaphoreType.REGULAR
    return pl.pallas_call(
        functools.partial(exchange, tp_count, grp_count),
        out_shape=(
            jax.ShapeDtypeStruct((layers, tensors, tp_count * rows, columns), flat_shards.dtype),
            jax.ShapeDtypeStruct((layers, share, columns), jnp.bfloat16),
        ),
        in_specs=[anywhere, pl.BlockSpec(memory_space=pltpu.SMEM), inside],
        out_specs=(anywhere, inside),
        scratch_shapes=[
            pltpu.VMEM((2, tp_count, WIDTH // LANES, shard, tensors, LANES), flat_shards.dtype),
            pltpu.VMEM((pairs, rows, shard * tensors), flat_shards.dtype),
            pltpu.VMEM((SLOTS, tp_count - 1, rows, chunk), flat_shards.dtype),
            pltpu.VMEM((SLOTS, tp_count * rows, chunk), flat_shards.dtype),
            pltpu.VMEM((grp_count, probe_count, chunk), jnp.float32),
            pltpu.VMEM((2, hops, 2, half, chunk), jnp.float32),
            pltpu.VMEM((2, hops, 2, half, chunk), jnp.float32),
            dma((2, tp_count, WIDTH // LANES)),
            dma((tp_count - 1, SLOTS)),
            dma((tp_count - 1, SLOTS)),
            regular((tp_count - 1,)),
            dma((SLOTS, tensors)),
            dma((2, hops, 2)),
            dma((2, hops, 2)),
            regular((2,)),
        ],
        compiler_params=pltpu.CompilerParams(
            collective_id=0, has_side_effects=True, vmem_limit_bytes=60 * 1024 * 1024
        ),
    )(flat_shards.transpose(0, 2, 1, 3), offsets, probes)


def solution(mesh):
    placed = (P(None, None, ("grp", "tp"), None), P(), P(None, "grp"))
    return jax.shard_map(
        per_device,
        mesh=mesh,
        in_specs=placed,
        out_specs=(P(None, None, "grp", "tp"), P(None, "grp", "tp")),
        check_vma=False,
    )
```

time: 708 us -> 620 us (0.88)
  Pallas kernels: 634 us -> 582 us
  local copies, waits for them, and re-layouts: 53.4 us -> 34.1 us
  other arithmetic: 13.2 us -> 0 us
    pallas_call x1 -> x0, Pallas kernels: 47.8 us -> none  [per_device(): pl.pallas_call(functools.partial(align, PAD), out_shape=jax.ShapeDtypeStr...]
    select_n x1 -> x0, other arithmetic: 9.71 us -> none  [per_device(): moved = jnp.where(starts[pair] == shift, shifts[shift], moved)]
    another operation x7 -> x0, local copies, waits for them, and re-layouts: 8.22 us -> none  [per_device(): main, rest = (jnp.stack(mains), jnp.stack(rests))]
    unnamed x11 -> x4, local copies, waits for them, and re-layouts: 38.9 us -> 34.1 us
where the time goes in v2:
time: 620 us; the launch traced here: 617 us
  Pallas kernels  582 us (94%)
  local copies, waits for them, and re-layouts  34.1 us (6%)
    pallas_call x1, Pallas kernels, per_device(): pl.pallas_call(functools.partial(exchange, tp_count, grp_count), out_shap...  582 us
    unnamed x4, local copies, waits for them, and re-layouts  34.1 us

profile of v2, /device:TPU:0, one launch (start us, length us, event | category | flops | bytes accessed | tf_op | source)
XLA Modules:
  0.0 616.8 jit_solution(13690764008728271918)
XLA Ops:
  0.6 582.1 %shard_map.50 = (bf16[2,2,1024,6144]{3,2,1,0:T(8,128)(2,1)}, bf16[2,64,6144]{2,1,0:T(8,128)(2,1)}) custom-call(bf16[2,258,2,24576]{3,2,1,0:T(2,128)(2,1)} %bitcast.1, s32[2,2]{1,0:T(2,128)} %offsets_ref.1, bf16[512,1024]{1,0:T(8,128)(2,1)} %probes_ref.1), custom_call_target="tpu_custom_call" | custom-call | tf_op jit(solution)/shard_map/pallas_call | solution.py:320
  582.7 0.0 copy-start
  582.7 33.0 %copy.7 = bf16[2,2,1024,6144]{3,2,1,0:T(8,128)(2,1)} copy(bf16[2,2,1024,6144]{3,2,1,0:T(8,128)(2,1)} %get-tuple-element.4) | data formatting | bytes 100663296
  615.7 0.0 copy-done
  615.7 1.1 copy.8
Async XLA Ops:
  582.7 33.0 %copy-start = (bf16[2,64,6144]{2,1,0:T(8,128)(2,1)S(1)}, bf16[2,64,6144]{2,1,0:T(8,128)(2,1)}, u32[]{:S(2)}) copy-start(bf16[2,64,6144]{2,1,0:T(8,128)(2,1)} %get-tuple-element.5) | copy-start | bytes 4718596

commit v3 on v2

--- a/solution.py
+++ b/solution.py
@@ -8,9 +8,9 @@
 from jax.sharding import PartitionSpec as P
 
 PAD = 2
-WIDTH = 256
+WIDTH = 128
 LANES = 128
-SLOTS = 4
+SLOTS = 6
 MESH = pl.DeviceIdType.MESH
 
 
@@ -62,7 +62,9 @@
     total = layers * per_layer
     share = probes_ref.shape[0] // grp_count
     half = share // 2
-    hops = grp_count - 1
+    hops = grp_count // 2
+    firsts = (slice(0, half), slice(half, share))
+    seconds = (slice(half, share), slice(0, half))
 
     def fetch(index, step, piece):
         layer, block = lax.div(index, per_layer), lax.rem(index, per_layer)
@@ -134,23 +136,30 @@
         )
 
     def ring_copy(way, stage, turn):
+        part = firsts[way] if stage == 0 else slice(0, share)
         return pltpu.make_async_remote_copy(
-            src_ref=outgoing.at[way, stage, turn],
-            dst_ref=incoming.at[way, stage, turn],
+            src_ref=outgoing.at[way, stage, turn, part],
+            dst_ref=incoming.at[way, stage, turn, part],
             send_sem=ring_send.at[way, stage, turn],
             recv_sem=ring_recv.at[way, stage, turn],
             device_id=(t, toward[way]),
             device_id_type=MESH,
         )
 
-    def own_rows(way, stage):
-        if way == 0:
-            owner = lax.rem(place + 2 * grp_count - 1 - stage, grp_count)
-        else:
-            owner = lax.rem(place + 1 + stage, grp_count)
-        first = ring_device(owner, grp_count) * share + way * half
-        return pl.ds(pl.multiple_of(first, half), half)
-
+    def own_rows(way, stage, part):
+        away = hops - stage
+        owner = lax.rem(place + (away if way == 0 else grp_count - away), grp_count)
+        first = ring_device(owner, grp_count) * share + part.start
+        size = part.stop - part.start
+        return pl.ds(pl.multiple_of(first, half), size)
+
+    barrier = pltpu.get_barrier_semaphore()
+    for step in range(1, tp_count):
+        pl.semaphore_signal(
+            barrier, inc=1, device_id=(lax.rem(t + step, tp_count), g), device_id_type=MESH
+        )
+    for way in range(2):
+        pl.semaphore_signal(barrier, inc=1, device_id=(t, toward[way]), device_id_type=MESH)
     fetch_all(0)
     fetch_all(1)
     at_row = lax.broadcasted_iota(jnp.int32, (rows, shard * tensors), 0)
@@ -161,14 +170,6 @@
             chosen[layer * tensors + tensor] = jnp.where(at_column == wanted, 1.0, 0.0).astype(
                 chosen.dtype
             )
-
-    barrier = pltpu.get_barrier_semaphore()
-    for step in range(1, tp_count):
-        pl.semaphore_signal(
-            barrier, inc=1, device_id=(lax.rem(t + step, tp_count), g), device_id_type=MESH
-        )
-    for way in range(2):
-        pl.semaphore_signal(barrier, inc=1, device_id=(t, toward[way]), device_id_type=MESH)
     pl.semaphore_wait(barrier, tp_count - 1 + 2)
 
     @pl.loop(0, SLOTS - 1)
@@ -193,7 +194,7 @@
 
             @pl.when(jnp.logical_and(index >= 0, index < total))
             def _():
-                place_of = lax.rem(index, grp_count)
+                place_of = lax.rem(index, hops)
                 if stage < hops:
 
                     @pl.when(index >= 2)
@@ -203,21 +204,27 @@
 
                     for way in range(2):
                         ring_copy(way, stage - 1, last_turn).wait_recv()
-                        outgoing[way, stage, turn] = (
-                            incoming[way, stage - 1, last_turn]
-                            + partial[place_of, own_rows(way, stage), :]
-                        )
+                        adds = (firsts[way],) if stage == 1 else firsts
+                        for part in adds:
+                            outgoing[way, stage, turn, part] = (
+                                incoming[way, stage - 1, last_turn, part]
+                                + partial[place_of, own_rows(way, stage, part), :]
+                            )
+                        if stage == 1:
+                            part = seconds[way]
+                            outgoing[way, stage, turn, part] = partial[
+                                place_of, own_rows(way, stage, part), :
+                            ]
                         ring_copy(way, stage, turn).start()
                 else:
                     layer, block = lax.div(index, per_layer), lax.rem(index, per_layer)
-                    parts = []
                     for way in range(2):
                         ring_copy(way, stage - 1, last_turn).wait_recv()
-                        parts.append(
-                            incoming[way, stage - 1, last_turn]
-                            + partial[place_of, own_rows(way, stage), :]
-                        )
-                    sums = jnp.concatenate(parts, axis=0)
+                    sums = (
+                        partial[place_of, own_rows(0, stage, slice(0, share)), :]
+                        + incoming[0, stage - 1, last_turn]
+                        + incoming[1, stage - 1, last_turn]
+                    )
                     gate, up = sums[:, :width], sums[:, width:]
                     hidden = gate / (1.0 + jnp.exp(-gate)) * up
                     where = pl.ds(pl.multiple_of(block * width, width), width)
@@ -226,7 +233,7 @@
         @pl.when(tick < total)
         def _():
             slot = lax.rem(tick, SLOTS)
-            kept = lax.rem(tick, grp_count)
+            kept = lax.rem(tick, hops)
             for step in range(1, tp_count):
                 x_arrival(tick, step).wait_recv()
             for tensor in range(tensors):
@@ -241,7 +248,8 @@
                     ring_copy(way, 0, turn).wait_send()
 
             for way in range(2):
-                outgoing[way, 0, turn] = partial[kept, own_rows(way, 0), :]
+                part = firsts[way]
+                outgoing[way, 0, turn, part] = partial[kept, own_rows(way, 0, part), :]
                 ring_copy(way, 0, turn).start()
 
         @pl.when(jnp.logical_and(tick >= 1, tick < total + hops - 2))
@@ -310,8 +318,7 @@
     probe_count = probes.shape[0]
     chunk = tensors * WIDTH
     share = probe_count // grp_count
-    half = share // 2
-    hops = grp_count - 1
+    hops = grp_count // 2
 
     anywhere = pl.BlockSpec(memory_space=pl.ANY)
     inside = pl.BlockSpec(memory_space=pltpu.VMEM)
@@ -330,9 +337,9 @@
             pltpu.VMEM((pairs, rows, shard * tensors), flat_shards.dtype),
             pltpu.VMEM((SLOTS, tp_count - 1, rows, chunk), flat_shards.dtype),
             pltpu.VMEM((SLOTS, tp_count * rows, chunk), flat_shards.dtype),
-            pltpu.VMEM((grp_count, probe_count, chunk), jnp.float32),
-            pltpu.VMEM((2, hops, 2, half, chunk), jnp.float32),
-            pltpu.VMEM((2, hops, 2, half, chunk), jnp.float32),
+            pltpu.VMEM((hops, probe_count, chunk), jnp.float32),
+            pltpu.VMEM((2, hops, 2, share, chunk), jnp.float32),
+            pltpu.VMEM((2, hops, 2, share, chunk), jnp.float32),
             dma((2, tp_count, WIDTH // LANES)),
             dma((tp_count - 1, SLOTS)),
             dma((tp_count - 1, SLOTS)),

time: 620 us -> 600 us (0.968)
  Pallas kernels: 582 us -> 565 us
    pallas_call x1, Pallas kernels: 582 us -> 565 us  [per_device(): pl.pallas_call(functools.partial(exchange, tp_count, grp_count), out_shap...]
where the time goes in v3:
time: 600 us
  Pallas kernels  565 us (94%)
  local copies, waits for them, and re-layouts  34.1 us (6%)
    pallas_call x1, Pallas kernels, per_device(): pl.pallas_call(functools.partial(exchange, tp_count, grp_count), out_shap...  565 us
    unnamed x4, local copies, waits for them, and re-layouts  34.1 us

profile of v3, /device:TPU:0, one launch (start us, length us, event | category | flops | bytes accessed | tf_op | source)
XLA Modules:
  0.0 599.8 jit_solution(5309450035516568640)
XLA Ops:
  0.6 565.1 %shard_map.50 = (bf16[2,2,1024,6144]{3,2,1,0:T(8,128)(2,1)}, bf16[2,64,6144]{2,1,0:T(8,128)(2,1)}) custom-call(bf16[2,258,2,24576]{3,2,1,0:T(2,128)(2,1)} %bitcast.1, s32[2,2]{1,0:T(2,128)} %offsets_ref.1, bf16[512,1024]{1,0:T(8,128)(2,1)} %probes_ref.1), custom_call_target="tpu_custom_call" | custom-call | tf_op jit(solution)/shard_map/pallas_call | solution.py:327
  565.7 0.0 copy-start
  565.7 33.0 %copy.7 = bf16[2,2,1024,6144]{3,2,1,0:T(8,128)(2,1)} copy(bf16[2,2,1024,6144]{3,2,1,0:T(8,128)(2,1)} %get-tuple-element.4) | data formatting | bytes 100663296
  598.7 0.0 copy-done
  598.7 1.1 copy.8
Async XLA Ops:
  565.7 33.0 %copy-start = (bf16[2,64,6144]{2,1,0:T(8,128)(2,1)S(1)}, bf16[2,64,6144]{2,1,0:T(8,128)(2,1)}, u32[]{:S(2)}) copy-start(bf16[2,64,6144]{2,1,0:T(8,128)(2,1)} %get-tuple-element.5) | copy-start | bytes 4718596
